TPU v7x, 32 devices: a whole 2x2x4 slice. The times are simulated.
32 devices in a mesh: section: 4 (over y, x), stem: 8 (over z, core).
Axes of the slice: x: 2, y: 2, z: 4, core: 2. Of those that a mesh axis runs over, the one named last changes fastest.
Arguments:
- bitstrings: int32 [4, 4, 32, 3], P('section'), may hold values 0 or 1
- boundary: float32 [2, 2048], replicated, may hold values from -6 to 6
- stem_tensor: float32 [4, 2, 2048, 8, 2048], P('section', None, 'stem'), may hold values from -0.09375 to 0.09375
- probe_vectors: float32 [4, 2, 2048], P('section'), may hold values from -0.09375 to 0.09375
- inbound_permutations: int32 [4, 2048], replicated, may hold values from 0 to 2047, each once within a row
Outputs:
- amplitudes: float32 [4, 2, 4, 32], P('section')
Inputs may be any that keep to these rules, and one draw needn't show every extreme that they name: `inbound_permutations`: each row of relabeling names every number of 0 to 2047 once.
All inputs are finite; a program needn't handle non-finite values. No bound on the sum of `bitstrings` on one device may be relied on, other than what follows from the above.
Results may differ from a plain program's by a relative error of at most 0.0003.
Values sent between devices are 32-bit elements; how exact they have to be, the bound alone decides.
No kernel may reach another device: no remote copies, remote signals or barrier semaphores. Data moves between devices by JAX's collectives and lax.ppermute only.
A program may use at most 128 MiB of HBM per device.

v0:
```python
import jax
import jax.numpy as jnp
from jax import lax
from jax.sharding import PartitionSpec as P


def from_behind(block, axis, distance):
    devices = range(lax.axis_size(axis))
    route = [(i - distance, i) for i in devices if i - distance in devices]
    return lax.ppermute(block, axis, route)


def local(bitstrings, boundary, stem_tensor, probe_vectors, inbound_permutations):
    section_count = lax.axis_size("section")
    segment_ordinal = lax.axis_index("section")
    stem_rank = lax.axis_index("stem")
    local_rows = stem_tensor.shape[2]
    settings_count = stem_tensor.shape[3]
    width = stem_tensor.shape[4]
    micro_count = bitstrings.shape[1]
    batch_size = bitstrings.shape[2]
    qubit_count = bitstrings.shape[3]
    powers = jnp.left_shift(jnp.int32(1), jnp.arange(qubit_count, dtype=jnp.int32))
    bit_patterns = jnp.sum(bitstrings[0] * powers, axis=-1)
    weight_real = stem_tensor[0, 0].reshape(local_rows * settings_count, width)
    weight_imag = stem_tensor[0, 1].reshape(local_rows * settings_count, width)
    own_perm = lax.dynamic_index_in_dim(inbound_permutations, segment_ordinal, 0, False)
    row_ids = lax.dynamic_slice_in_dim(own_perm, stem_rank * local_rows, local_rows)
    start_state = jnp.broadcast_to(
        jnp.take(boundary, row_ids, axis=1)[:, None, :], (2, batch_size, local_rows)
    )
    probe_re = probe_vectors[0, 0]
    probe_im = probe_vectors[0, 1]
    setting_ids = jnp.arange(settings_count, dtype=jnp.int32)

    def advance(moment, state_pair):
        incoming, buffer = state_pair
        position = moment - segment_ordinal
        active = jnp.logical_and(position >= 0, position < micro_count)
        clipped = jnp.clip(position, 0, micro_count - 1)
        pattern = lax.dynamic_index_in_dim(bit_patterns, clipped, 0, False)
        gathered = lax.all_gather(incoming, "stem", axis=2, tiled=True)
        arriving = jnp.take(gathered, row_ids, axis=2)
        current = jnp.where(segment_ordinal == 0, start_state, arriving)
        onehot = (setting_ids[None, :] == pattern[:, None]).astype(jnp.float32)
        expanded = (current[:, :, :, None] * onehot[None, :, None, :]).reshape(
            2 * batch_size, local_rows * settings_count
        )
        prod_real = jnp.dot(expanded, weight_real, precision=lax.Precision.HIGHEST)
        prod_imag = jnp.dot(expanded, weight_imag, precision=lax.Precision.HIGHEST)
        out_real = prod_real[:batch_size] - prod_imag[batch_size:]
        out_imag = prod_imag[:batch_size] + prod_real[batch_size:]
        partial_value = jnp.stack([out_real, out_imag])
        term_real = jnp.dot(out_real, probe_re, precision=lax.Precision.HIGHEST) - jnp.dot(
            out_imag, probe_im, precision=lax.Precision.HIGHEST
        )
        term_imag = jnp.dot(out_real, probe_im, precision=lax.Precision.HIGHEST) + jnp.dot(
            out_imag, probe_re, precision=lax.Precision.HIGHEST
        )
        intersection_terms = jnp.stack([term_real, term_imag])[:, None, :]
        previous = lax.dynamic_slice_in_dim(buffer, clipped, 1, 1)
        updated = jnp.where(active, intersection_terms, previous)
        buffer = lax.dynamic_update_slice_in_dim(buffer, updated, clipped, 1)
        summed = lax.psum_scatter(partial_value, "stem", scatter_dimension=2, tiled=True)
        incoming = from_behind(summed, "section", 1)
        return (incoming, buffer)

    initial_incoming = jnp.zeros((2, batch_size, local_rows), jnp.float32)
    first_buffer = jnp.zeros((2, micro_count, batch_size), jnp.float32)
    time_steps = micro_count + section_count - 1
    final_incoming, buffer = lax.fori_loop(0, time_steps, advance, (initial_incoming, first_buffer))
    amplitudes = lax.psum(buffer, "stem")
    return amplitudes[None]


def solution(mesh):
    return jax.shard_map(
        local,
        mesh=mesh,
        in_specs=(
            P("section", None, None, None),
            P(),
            P("section", None, "stem", None, None),
            P("section", None, None),
            P(),
        ),
        out_specs=P("section", None, None, None),
        check_vma=False,
    )
```

profile of v0, /device:TPU:5, one launch (start us, length us, event | category | flops | bytes accessed | tf_op | source)
XLA Modules:
  0.0 622.9 jit_solution(6774410743164879172)
XLA Ops:
  7.3 1.1 copy.13
  9.3 21.2 %slice_bitcast_fusion = (f32[2048,2048]{1,0:T(8,128)}, f32[2048,2048]{1,0:T(8,128)}) fusion(f32[1,2,256,8,2048]{4,3,2,1,0:T(8,128)} %param.9), kind=kLoop, calls=%fused_computation.29 | loop fusion | bytes 67108864 | tf_op jit(solution)/shard_map/reshape;squeeze | solution.py:26
  30.6 567.1 %while.17 = (s32[]{:T(128)}, f32[2,32,256]{2,1,0:T(8,128)S(1)}, f32[2,4,32]{2,1,0:T(4,128)S(1)}, pred[]{:T(512)}, s32[256]{0:T(256)S(1)}, /*index=5*/s32[]{:T(12...) while((s32[]{:T(128)}, f32[2,32,256]{2,1,0:T(8,128)S(1)}, ...), condition=%wide.region_3.4_spmd.clone, body=%wide.region_1.3_spmd.clone.sunk | while | flops 6446288896 | bytes 113100216 | solution.py:71
  30.7 15.6 %all_gather.10 = f32[2,32,2048]{2,1,0:T(8,128)S(1)} all-gather(f32[2,32,256]{2,1,0:T(8,128)S(1)} %get-tuple-element.424), channel_id=1, replica_groups=mesh['section'=4,'stem'=8] {'stem'}, dimensions={2}, use_global_device_ids=true | all-gather | bytes 589824 | tf_op jit(solution)/shard_map/while/body/eval_jaxpr/all_gather | solution.py:42
  46.3 1.0 copy.19
  48.3 1.1 bitcast_select_fusion.2
  50.1 1.1 mul.72
  51.3 13.9 %fusion.48 = f32[64,2048]{1,0:T(8,128)S(1)} fusion(f32[64,2048]{0,1:T(8,128)S(1)} %mul.72, f32[2048,2048]{1,0:T(8,128)} %get-tuple-element.447), kind=kOutput, calls=%fused_computation.41.clone.1 | convolution fusion | flops 3221225472 | bytes 17825792 | tf_op jit(solution)/shard_map/while/body/eval_jaxpr/dot_general | solution.py:50
  65.2 10.2 %fusion.49 = f32[64,2048]{1,0:T(8,128)S(1)} fusion(f32[64,2048]{0,1:T(8,128)S(1)} %mul.72, f32[2048,2048]{1,0:T(8,128)S(1)} %copy-done), kind=kOutput, calls=%fused_computation.40.clone.1 | convolution fusion | flops 3221225472 | bytes 17825792 | tf_op jit(solution)/shard_map/while/body/eval_jaxpr/dot_general | solution.py:49
  77.7 27.5 %reduce-scatter.2.cloned.1.call-done = f32[2,32,256]{2,1,0:T(8,128)} async-done(((f32[2,32,2048]{2,1,0:T(8,128)}), f32[2,32,256]{2,1,0:T(8,128)}) %reduce-scatter.2.cloned.1.call-update) | async-done | bytes 65552 | tf_op jit(solution)/shard_map/while/body/eval_jaxpr/reduce_scatter | solution.py:64
  105.1 3.2 collective-permute-start
  108.4 2.9 collective-permute-done
  111.3 19.5 %all_gather.10 = f32[2,32,2048]{2,1,0:T(8,128)S(1)} all-gather(f32[2,32,256]{2,1,0:T(8,128)S(1)} %get-tuple-element.424), channel_id=1, replica_groups=mesh['section'=4,'stem'=8] {'stem'}, dimensions={2}, use_global_device_ids=true | all-gather | bytes 589824 | tf_op jit(solution)/shard_map/while/body/eval_jaxpr/all_gather | solution.py:42
  132.8 1.1 bitcast_select_fusion.2
  134.6 1.1 mul.72
  135.8 13.9 %fusion.48 = f32[64,2048]{1,0:T(8,128)S(1)} fusion(f32[64,2048]{0,1:T(8,128)S(1)} %mul.72, f32[2048,2048]{1,0:T(8,128)} %get-tuple-element.447), kind=kOutput, calls=%fused_computation.41.clone.1 | convolution fusion | flops 3221225472 | bytes 17825792 | tf_op jit(solution)/shard_map/while/body/eval_jaxpr/dot_general | solution.py:50
  149.7 10.2 %fusion.49 = f32[64,2048]{1,0:T(8,128)S(1)} fusion(f32[64,2048]{0,1:T(8,128)S(1)} %mul.72, f32[2048,2048]{1,0:T(8,128)S(1)} %copy-done), kind=kOutput, calls=%fused_computation.40.clone.1 | convolution fusion | flops 3221225472 | bytes 17825792 | tf_op jit(solution)/shard_map/while/body/eval_jaxpr/dot_general | solution.py:49
  162.2 24.0 %reduce-scatter.2.cloned.1.call-done = f32[2,32,256]{2,1,0:T(8,128)} async-done(((f32[2,32,2048]{2,1,0:T(8,128)}), f32[2,32,256]{2,1,0:T(8,128)}) %reduce-scatter.2.cloned.1.call-update) | async-done | bytes 65552 | tf_op jit(solution)/shard_map/while/body/eval_jaxpr/reduce_scatter | solution.py:64
  186.2 3.1 collective-permute-start
  189.3 2.9 collective-permute-done
  192.3 19.5 %all_gather.10 = f32[2,32,2048]{2,1,0:T(8,128)S(1)} all-gather(f32[2,32,256]{2,1,0:T(8,128)S(1)} %get-tuple-element.424), channel_id=1, replica_groups=mesh['section'=4,'stem'=8] {'stem'}, dimensions={2}, use_global_device_ids=true | all-gather | bytes 589824 | tf_op jit(solution)/shard_map/while/body/eval_jaxpr/all_gather | solution.py:42
  211.8 1.0 copy.19
  213.8 1.1 bitcast_select_fusion.2
  215.6 1.1 mul.72
  216.8 13.9 %fusion.48 = f32[64,2048]{1,0:T(8,128)S(1)} fusion(f32[64,2048]{0,1:T(8,128)S(1)} %mul.72, f32[2048,2048]{1,0:T(8,128)} %get-tuple-element.447), kind=kOutput, calls=%fused_computation.41.clone.1 | convolution fusion | flops 3221225472 | bytes 17825792 | tf_op jit(solution)/shard_map/while/body/eval_jaxpr/dot_general | solution.py:50
  230.7 10.2 %fusion.49 = f32[64,2048]{1,0:T(8,128)S(1)} fusion(f32[64,2048]{0,1:T(8,128)S(1)} %mul.72, f32[2048,2048]{1,0:T(8,128)S(1)} %copy-done), kind=kOutput, calls=%fused_computation.40.clone.1 | convolution fusion | flops 3221225472 | bytes 17825792 | tf_op jit(solution)/shard_map/while/body/eval_jaxpr/dot_general | solution.py:49
  243.2 24.1 %reduce-scatter.2.cloned.1.call-done = f32[2,32,256]{2,1,0:T(8,128)} async-done(((f32[2,32,2048]{2,1,0:T(8,128)}), f32[2,32,256]{2,1,0:T(8,128)}) %reduce-scatter.2.cloned.1.call-update) | async-done | bytes 65552 | tf_op jit(solution)/shard_map/while/body/eval_jaxpr/reduce_scatter | solution.py:64
  267.3 2.9 collective-permute-start
  270.3 3.1 collective-permute-done
  273.5 19.5 %all_gather.10 = f32[2,32,2048]{2,1,0:T(8,128)S(1)} all-gather(f32[2,32,256]{2,1,0:T(8,128)S(1)} %get-tuple-element.424), channel_id=1, replica_groups=mesh['section'=4,'stem'=8] {'stem'}, dimensions={2}, use_global_device_ids=true | all-gather | bytes 589824 | tf_op jit(solution)/shard_map/while/body/eval_jaxpr/all_gather | solution.py:42
  295.0 1.1 bitcast_select_fusion.2
  296.8 1.1 mul.72
  298.0 13.9 %fusion.48 = f32[64,2048]{1,0:T(8,128)S(1)} fusion(f32[64,2048]{0,1:T(8,128)S(1)} %mul.72, f32[2048,2048]{1,0:T(8,128)} %get-tuple-element.447), kind=kOutput, calls=%fused_computation.41.clone.1 | convolution fusion | flops 3221225472 | bytes 17825792 | tf_op jit(solution)/shard_map/while/body/eval_jaxpr/dot_general | solution.py:50
  311.9 10.2 %fusion.49 = f32[64,2048]{1,0:T(8,128)S(1)} fusion(f32[64,2048]{0,1:T(8,128)S(1)} %mul.72, f32[2048,2048]{1,0:T(8,128)S(1)} %copy-done), kind=kOutput, calls=%fused_computation.40.clone.1 | convolution fusion | flops 3221225472 | bytes 17825792 | tf_op jit(solution)/shard_map/while/body/eval_jaxpr/dot_general | solution.py:49
  324.4 24.0 %reduce-scatter.2.cloned.1.call-done = f32[2,32,256]{2,1,0:T(8,128)} async-done(((f32[2,32,2048]{2,1,0:T(8,128)}), f32[2,32,256]{2,1,0:T(8,128)}) %reduce-scatter.2.cloned.1.call-update) | async-done | bytes 65552 | tf_op jit(solution)/shard_map/while/body/eval_jaxpr/reduce_scatter | solution.py:64
  348.4 3.1 collective-permute-start
  351.6 2.9 collective-permute-done
  354.5 19.5 %all_gather.10 = f32[2,32,2048]{2,1,0:T(8,128)S(1)} all-gather(f32[2,32,256]{2,1,0:T(8,128)S(1)} %get-tuple-element.424), channel_id=1, replica_groups=mesh['section'=4,'stem'=8] {'stem'}, dimensions={2}, use_global_device_ids=true | all-gather | bytes 589824 | tf_op jit(solution)/shard_map/while/body/eval_jaxpr/all_gather | solution.py:42
  374.0 1.0 copy.19
  376.1 1.1 bitcast_select_fusion.2
  377.9 1.1 mul.72
  379.0 13.9 %fusion.48 = f32[64,2048]{1,0:T(8,128)S(1)} fusion(f32[64,2048]{0,1:T(8,128)S(1)} %mul.72, f32[2048,2048]{1,0:T(8,128)} %get-tuple-element.447), kind=kOutput, calls=%fused_computation.41.clone.1 | convolution fusion | flops 3221225472 | bytes 17825792 | tf_op jit(solution)/shard_map/while/body/eval_jaxpr/dot_general | solution.py:50
  392.9 10.2 %fusion.49 = f32[64,2048]{1,0:T(8,128)S(1)} fusion(f32[64,2048]{0,1:T(8,128)S(1)} %mul.72, f32[2048,2048]{1,0:T(8,128)S(1)} %copy-done), kind=kOutput, calls=%fused_computation.40.clone.1 | convolution fusion | flops 3221225472 | bytes 17825792 | tf_op jit(solution)/shard_map/while/body/eval_jaxpr/dot_general | solution.py:49
  405.4 24.1 %reduce-scatter.2.cloned.1.call-done = f32[2,32,256]{2,1,0:T(8,128)} async-done(((f32[2,32,2048]{2,1,0:T(8,128)}), f32[2,32,256]{2,1,0:T(8,128)}) %reduce-scatter.2.cloned.1.call-update) | async-done | bytes 65552 | tf_op jit(solution)/shard_map/while/body/eval_jaxpr/reduce_scatter | solution.py:64
  429.5 3.1 collective-permute-start
  432.7 2.9 collective-permute-done
  435.7 19.5 %all_gather.10 = f32[2,32,2048]{2,1,0:T(8,128)S(1)} all-gather(f32[2,32,256]{2,1,0:T(8,128)S(1)} %get-tuple-element.424), channel_id=1, replica_groups=mesh['section'=4,'stem'=8] {'stem'}, dimensions={2}, use_global_device_ids=true | all-gather | bytes 589824 | tf_op jit(solution)/shard_map/while/body/eval_jaxpr/all_gather | solution.py:42
  457.2 1.1 bitcast_select_fusion.2
  459.0 1.1 mul.72
  460.2 13.9 %fusion.48 = f32[64,2048]{1,0:T(8,128)S(1)} fusion(f32[64,2048]{0,1:T(8,128)S(1)} %mul.72, f32[2048,2048]{1,0:T(8,128)} %get-tuple-element.447), kind=kOutput, calls=%fused_computation.41.clone.1 | convolution fusion | flops 3221225472 | bytes 17825792 | tf_op jit(solution)/shard_map/while/body/eval_jaxpr/dot_general | solution.py:50
  474.1 10.2 %fusion.49 = f32[64,2048]{1,0:T(8,128)S(1)} fusion(f32[64,2048]{0,1:T(8,128)S(1)} %mul.72, f32[2048,2048]{1,0:T(8,128)S(1)} %copy-done), kind=kOutput, calls=%fused_computation.40.clone.1 | convolution fusion | flops 3221225472 | bytes 17825792 | tf_op jit(solution)/shard_map/while/body/eval_jaxpr/dot_general | solution.py:49
  486.6 24.0 %reduce-scatter.2.cloned.1.call-done = f32[2,32,256]{2,1,0:T(8,128)} async-done(((f32[2,32,2048]{2,1,0:T(8,128)}), f32[2,32,256]{2,1,0:T(8,128)}) %reduce-scatter.2.cloned.1.call-update) | async-done | bytes 65552 | tf_op jit(solution)/shard_map/while/body/eval_jaxpr/reduce_scatter | solution.py:64
  510.6 3.1 collective-permute-start
  513.7 2.9 collective-permute-done
  516.7 19.5 %all_gather.10 = f32[2,32,2048]{2,1,0:T(8,128)S(1)} all-gather(f32[2,32,256]{2,1,0:T(8,128)S(1)} %get-tuple-element.424), channel_id=1, replica_groups=mesh['section'=4,'stem'=8] {'stem'}, dimensions={2}, use_global_device_ids=true | all-gather | bytes 589824 | tf_op jit(solution)/shard_map/while/body/eval_jaxpr/all_gather | solution.py:42
  536.2 1.0 copy.19
  538.2 1.1 bitcast_select_fusion.2
  540.0 1.1 mul.72
  541.2 13.9 %fusion.48 = f32[64,2048]{1,0:T(8,128)S(1)} fusion(f32[64,2048]{0,1:T(8,128)S(1)} %mul.72, f32[2048,2048]{1,0:T(8,128)} %get-tuple-element.447), kind=kOutput, calls=%fused_computation.41.clone.1 | convolution fusion | flops 3221225472 | bytes 17825792 | tf_op jit(solution)/shard_map/while/body/eval_jaxpr/dot_general | solution.py:50
  555.1 10.2 %fusion.49 = f32[64,2048]{1,0:T(8,128)S(1)} fusion(f32[64,2048]{0,1:T(8,128)S(1)} %mul.72, f32[2048,2048]{1,0:T(8,128)S(1)} %copy-done), kind=kOutput, calls=%fused_computation.40.clone.1 | convolution fusion | flops 3221225472 | bytes 17825792 | tf_op jit(solution)/shard_map/while/body/eval_jaxpr/dot_general | solution.py:49
  567.6 24.0 %reduce-scatter.2.cloned.1.call-done = f32[2,32,256]{2,1,0:T(8,128)} async-done(((f32[2,32,2048]{2,1,0:T(8,128)}), f32[2,32,256]{2,1,0:T(8,128)}) %reduce-scatter.2.cloned.1.call-update) | async-done | bytes 65552 | tf_op jit(solution)/shard_map/while/body/eval_jaxpr/reduce_scatter | solution.py:64
  591.6 3.1 collective-permute-start
  594.8 2.9 collective-permute-done
  597.7 18.4 %psum.7 = f32[1,2,4,32]{3,2,1,0:T(4,128)} all-reduce(f32[1,2,4,32]{3,2,1,0:T(4,128)S(1)} %bitcast.124), channel_id=1, replica_groups=mesh['section'=4,'stem'=8] {'stem'}, use_global_device_ids=true, to_apply=%region_4.5 | all-reduce | flops 256 | bytes 2048 | tf_op jit(solution)/shard_map/psum | solution.py:72
  (157 shorter events, 33.0 us)
Async XLA Ops:
  9.3 21.2 %copy-start.1 = (f32[1,2,2048]{2,1,0:T(2,128)S(1)}, f32[1,2,2048]{2,1,0:T(2,128)}, u32[]{:S(2)}) copy-start(f32[1,2,2048]{2,1,0:T(2,128)} %param.10) | copy-start | bytes 49156
  9.3 21.2 %copy-start.2 = (s32[1,4,32,3]{2,1,3,0:T(4,128)S(1)}, s32[1,4,32,3]{2,1,3,0:T(4,128)}, u32[]{:S(2)}) copy-start(s32[1,4,32,3]{2,1,3,0:T(4,128)} %param.7) | copy-start | bytes 4612
  30.6 74.5 %reduce-scatter.2.cloned.1.call-start = ((), (), s32[]{:S(2)}) async-start(), calls=%async_computation.1 | async-start | bytes 589824 | tf_op jit(solution)/shard_map/while/body/eval_jaxpr/reduce_scatter | solution.py:64
  51.2 13.9 %copy-start = (f32[2048,2048]{1,0:T(8,128)S(1)}, f32[2048,2048]{1,0:T(8,128)}, u32[]{:S(2)}) copy-start(f32[2048,2048]{1,0:T(8,128)} %get-tuple-element.446) | copy-start | bytes 50331652 | tf_op jit(solution)/shard_map/while
  105.1 6.1 collective-permute-start
  111.2 74.9 %reduce-scatter.2.cloned.1.call-start = ((), (), s32[]{:S(2)}) async-start(), calls=%async_computation.1 | async-start | bytes 589824 | tf_op jit(solution)/shard_map/while/body/eval_jaxpr/reduce_scatter | solution.py:64
  135.8 13.9 %copy-start = (f32[2048,2048]{1,0:T(8,128)S(1)}, f32[2048,2048]{1,0:T(8,128)}, u32[]{:S(2)}) copy-start(f32[2048,2048]{1,0:T(8,128)} %get-tuple-element.446) | copy-start | bytes 50331652 | tf_op jit(solution)/shard_map/while
  186.2 6.1 collective-permute-start
  192.3 75.1 %reduce-scatter.2.cloned.1.call-start = ((), (), s32[]{:S(2)}) async-start(), calls=%async_computation.1 | async-start | bytes 589824 | tf_op jit(solution)/shard_map/while/body/eval_jaxpr/reduce_scatter | solution.py:64
  216.8 13.9 %copy-start = (f32[2048,2048]{1,0:T(8,128)S(1)}, f32[2048,2048]{1,0:T(8,128)}, u32[]{:S(2)}) copy-start(f32[2048,2048]{1,0:T(8,128)} %get-tuple-element.446) | copy-start | bytes 50331652 | tf_op jit(solution)/shard_map/while
  267.3 6.1 collective-permute-start
  273.4 74.9 %reduce-scatter.2.cloned.1.call-start = ((), (), s32[]{:S(2)}) async-start(), calls=%async_computation.1 | async-start | bytes 589824 | tf_op jit(solution)/shard_map/while/body/eval_jaxpr/reduce_scatter | solution.py:64
  298.0 13.9 %copy-start = (f32[2048,2048]{1,0:T(8,128)S(1)}, f32[2048,2048]{1,0:T(8,128)}, u32[]{:S(2)}) copy-start(f32[2048,2048]{1,0:T(8,128)} %get-tuple-element.446) | copy-start | bytes 50331652 | tf_op jit(solution)/shard_map/while
  348.4 6.1 collective-permute-start
  354.5 75.1 %reduce-scatter.2.cloned.1.call-start = ((), (), s32[]{:S(2)}) async-start(), calls=%async_computation.1 | async-start | bytes 589824 | tf_op jit(solution)/shard_map/while/body/eval_jaxpr/reduce_scatter | solution.py:64
  379.0 13.9 %copy-start = (f32[2048,2048]{1,0:T(8,128)S(1)}, f32[2048,2048]{1,0:T(8,128)}, u32[]{:S(2)}) copy-start(f32[2048,2048]{1,0:T(8,128)} %get-tuple-element.446) | copy-start | bytes 50331652 | tf_op jit(solution)/shard_map/while
  429.5 6.1 collective-permute-start
  435.6 74.9 %reduce-scatter.2.cloned.1.call-start = ((), (), s32[]{:S(2)}) async-start(), calls=%async_computation.1 | async-start | bytes 589824 | tf_op jit(solution)/shard_map/while/body/eval_jaxpr/reduce_scatter | solution.py:64
  460.2 13.9 %copy-start = (f32[2048,2048]{1,0:T(8,128)S(1)}, f32[2048,2048]{1,0:T(8,128)}, u32[]{:S(2)}) copy-start(f32[2048,2048]{1,0:T(8,128)} %get-tuple-element.446) | copy-start | bytes 50331652 | tf_op jit(solution)/shard_map/while
  510.6 6.1 collective-permute-start
  516.7 74.9 %reduce-scatter.2.cloned.1.call-start = ((), (), s32[]{:S(2)}) async-start(), calls=%async_computation.1 | async-start | bytes 589824 | tf_op jit(solution)/shard_map/while/body/eval_jaxpr/reduce_scatter | solution.py:64
  541.2 13.9 %copy-start = (f32[2048,2048]{1,0:T(8,128)S(1)}, f32[2048,2048]{1,0:T(8,128)}, u32[]{:S(2)}) copy-start(f32[2048,2048]{1,0:T(8,128)} %get-tuple-element.446) | copy-start | bytes 50331652 | tf_op jit(solution)/shard_map/while
  591.6 6.1 collective-permute-start
Sparse Core Ops, SparseCore 0:
  76.4 28.6 reduce-scatter.1
  161.0 25.1 reduce-scatter.1
  242.0 25.2 reduce-scatter.1
  323.2 25.1 reduce-scatter.1
  404.2 25.2 reduce-scatter.1
  485.3 25.1 reduce-scatter.1
  566.4 25.1 reduce-scatter.1
where the time goes:
time: 623 us
  waiting for transfers between devices  192 us (31%)
  matrix products  178 us (29%)
  blocking collectives  151 us (24%)
  local copies, waits for them, and re-layouts  45.5 us (7%)
  starting transfers between devices  21.7 us (3%)
  other arithmetic  20 us (3%)
  between operations  13.5 us (2%)
    reduce_scatter x7, waiting for transfers between devices, advance(): lax.psum_scatter(partial_value, 'stem', scatter_dimension=2, tiled=True)  172 us
    all_gather x7, blocking collectives, advance(): gathered = lax.all_gather(incoming, 'stem', axis=2, tiled=True)  133 us
    dot_general x7, matrix products, advance(): prod_imag = jnp.dot(expanded, weight_imag, precision=lax.Precision.HIGHEST)  97.4 us
    dot_general x7, matrix products, advance(): prod_real = jnp.dot(expanded, weight_real, precision=lax.Precision.HIGHEST)  71.4 us
    ppermute x7, starting transfers between devices, from_behind(): return lax.ppermute(block, axis, route)  21.7 us
    another operation x1, local copies, waits for them, and re-layouts, local(): weight_imag = stem_tensor[0, 1].reshape(local_rows * settings_count, width)  21.2 us
    ppermute x7, waiting for transfers between devices, from_behind(): return lax.ppermute(block, axis, route)  20.6 us
    psum x1, blocking collectives, local(): amplitudes = lax.psum(buffer, 'stem')  18.4 us
  transfers between devices with their start and end apart: 14, of which 14 were waited for; matrix products, arithmetic and copies ran while one was open for 2% of the time, Pallas kernels for 0%

commit v1 on v0

--- a/solution.py
+++ b/solution.py
@@ -39,7 +39,14 @@
         active = jnp.logical_and(position >= 0, position < micro_count)
         clipped = jnp.clip(position, 0, micro_count - 1)
         pattern = lax.dynamic_index_in_dim(bit_patterns, clipped, 0, False)
-        gathered = lax.all_gather(incoming, "stem", axis=2, tiled=True)
+        ring = [incoming]
+        for hop in range(7):
+            ring.append(lax.ppermute(ring[-1], "stem", [(dev, (dev + 1) % 8) for dev in range(8)]))
+        gathered = jnp.roll(
+            jnp.concatenate(ring[::-1], axis=2),
+            (lax.axis_index("stem") + 1) * ring[0].shape[2],
+            axis=2,
+        )
         arriving = jnp.take(gathered, row_ids, axis=2)
         current = jnp.where(segment_ordinal == 0, start_state, arriving)
         onehot = (setting_ids[None, :] == pattern[:, None]).astype(jnp.float32)

time: 623 us -> 786 us (1.26)
  waiting for transfers between devices: 192 us -> 461 us
  blocking collectives: 151 us -> 18.5 us
  starting transfers between devices: 21.7 us -> 46.3 us
    ppermute x0 -> x49, waiting for transfers between devices: none -> 241 us  [advance(): lax.ppermute(ring[-1], 'stem', [(dev, (dev + 1) % 8) for dev in range(8)])]
    all_gather x7 -> x0, blocking collectives: 133 us -> none  [advance(): gathered = lax.all_gather(incoming, 'stem', axis=2, tiled=True)]
    reduce_scatter x7, waiting for transfers between devices: 172 us -> 199 us  [advance(): lax.psum_scatter(partial_value, 'stem', scatter_dimension=2, tiled=True)]
    ppermute x0 -> x49, starting transfers between devices: none -> 24.6 us  [advance(): lax.ppermute(ring[-1], 'stem', [(dev, (dev + 1) % 8) for dev in range(8)])]
    while x14 -> x126, local copies, waits for them, and re-layouts: 0.03 us -> 8.09 us
  transfers between devices with their start and end apart: 14 -> 63, of which waited for: 14 -> 63; matrix products, arithmetic and copies ran while one was open for 2% -> 1% of each run, Pallas kernels for 0% -> 0%
where the time goes in v1:
time: 786 us; the launch traced here: 785 us
  waiting for transfers between devices  461 us (59%)
  matrix products  178 us (23%)
  local copies, waits for them, and re-layouts  46.7 us (6%)
  starting transfers between devices  46.3 us (6%)
  other arithmetic  20.1 us (3%)
  blocking collectives  18.5 us (2%)
  between operations  13.5 us (2%)
    ppermute x49, waiting for transfers between devices, advance(): lax.ppermute(ring[-1], 'stem', [(dev, (dev + 1) % 8) for dev in range(8)])  241 us
    reduce_scatter x7, waiting for transfers between devices, advance(): lax.psum_scatter(partial_value, 'stem', scatter_dimension=2, tiled=True)  199 us
    dot_general x7, matrix products, advance(): prod_imag = jnp.dot(expanded, weight_imag, precision=lax.Precision.HIGHEST)  97.4 us
    dot_general x7, matrix products, advance(): prod_real = jnp.dot(expanded, weight_real, precision=lax.Precision.HIGHEST)  71.4 us
    ppermute x49, starting transfers between devices, advance(): lax.ppermute(ring[-1], 'stem', [(dev, (dev + 1) % 8) for dev in range(8)])  24.6 us
    ppermute x7, starting transfers between devices, from_behind(): return lax.ppermute(block, axis, route)  21.7 us
    another operation x1, local copies, waits for them, and re-layouts, local(): weight_imag = stem_tensor[0, 1].reshape(local_rows * settings_count, width)  21.2 us
    ppermute x7, waiting for transfers between devices, from_behind(): return lax.ppermute(block, axis, route)  20.6 us
  transfers between devices with their start and end apart: 63, of which 63 were waited for; matrix products, arithmetic and copies ran while one was open for 1% of the time, Pallas kernels for 0%

profile of v1, /device:TPU:5, one launch (start us, length us, event | category | flops | bytes accessed | tf_op | source)
XLA Modules:
  0.0 785.3 jit_solution(15490271923993913424)
XLA Ops:
  9.3 21.2 %slice_bitcast_fusion = (f32[2048,2048]{1,0:T(8,128)}, f32[2048,2048]{1,0:T(8,128)}) fusion(f32[1,2,256,8,2048]{4,3,2,1,0:T(8,128)} %param.9), kind=kLoop, calls=%fused_computation.47 | loop fusion | bytes 67108864 | tf_op jit(solution)/shard_map/reshape;squeeze | solution.py:26
  30.6 729.4 %while.18 = (s32[]{:T(128)}, f32[2,32,256]{2,1,0:T(8,128)S(1)}, f32[2,4,32]{2,1,0:T(4,128)S(1)}, pred[]{:T(512)}, s32[256]{0:T(256)S(1)}, /*index=5*/s32[]{:T(12...) while((s32[]{:T(128)}, f32[2,32,256]{2,1,0:T(8,128)S(1)}, ...), condition=%wide.region_3.4_spmd.clone, body=%wide.region_1.3_spmd.clone.sunk | while | flops 6446288896 | bytes 117491664 | solution.py:78
  43.6 5.0 collective-permute-done.3
  48.6 5.5 collective-permute-done.4
  54.1 5.5 collective-permute-done.5
  59.6 5.5 collective-permute-done.6
  70.3 13.9 %fusion.51 = f32[64,2048]{1,0:T(8,128)S(1)} fusion(f32[64,2048]{0,1:T(8,128)S(1)} %mul.87, f32[2048,2048]{1,0:T(8,128)} %get-tuple-element.499), kind=kOutput, calls=%fused_computation.59.clone.1 | convolution fusion | flops 3221225472 | bytes 17825792 | tf_op jit(solution)/shard_map/while/body/eval_jaxpr/dot_general | solution.py:57
  84.3 10.2 %fusion.52 = f32[64,2048]{1,0:T(8,128)S(1)} fusion(f32[64,2048]{0,1:T(8,128)S(1)} %mul.87, f32[2048,2048]{1,0:T(8,128)S(1)} %copy-done), kind=kOutput, calls=%fused_computation.58.clone.1 | convolution fusion | flops 3221225472 | bytes 17825792 | tf_op jit(solution)/shard_map/while/body/eval_jaxpr/dot_general | solution.py:56
  96.8 29.2 %reduce-scatter.2.cloned.1.call-done = f32[2,32,256]{2,1,0:T(8,128)} async-done(((f32[2,32,2048]{2,1,0:T(8,128)}), f32[2,32,256]{2,1,0:T(8,128)}) %reduce-scatter.2.cloned.1.call-update) | async-done | bytes 65552 | tf_op jit(solution)/shard_map/while/body/eval_jaxpr/reduce_scatter | solution.py:71
  138.2 5.0 collective-permute-done.1
  143.2 5.5 collective-permute-done.2
  148.7 5.5 collective-permute-done.3
  154.2 5.5 collective-permute-done.4
  159.7 5.5 collective-permute-done.5
  165.2 5.5 collective-permute-done.6
  175.9 13.9 %fusion.51 = f32[64,2048]{1,0:T(8,128)S(1)} fusion(f32[64,2048]{0,1:T(8,128)S(1)} %mul.87, f32[2048,2048]{1,0:T(8,128)} %get-tuple-element.499), kind=kOutput, calls=%fused_computation.59.clone.1 | convolution fusion | flops 3221225472 | bytes 17825792 | tf_op jit(solution)/shard_map/while/body/eval_jaxpr/dot_general | solution.py:57
  189.9 10.2 %fusion.52 = f32[64,2048]{1,0:T(8,128)S(1)} fusion(f32[64,2048]{0,1:T(8,128)S(1)} %mul.87, f32[2048,2048]{1,0:T(8,128)S(1)} %copy-done), kind=kOutput, calls=%fused_computation.58.clone.1 | convolution fusion | flops 3221225472 | bytes 17825792 | tf_op jit(solution)/shard_map/while/body/eval_jaxpr/dot_general | solution.py:56
  202.3 28.3 %reduce-scatter.2.cloned.1.call-done = f32[2,32,256]{2,1,0:T(8,128)} async-done(((f32[2,32,2048]{2,1,0:T(8,128)}), f32[2,32,256]{2,1,0:T(8,128)}) %reduce-scatter.2.cloned.1.call-update) | async-done | bytes 65552 | tf_op jit(solution)/shard_map/while/body/eval_jaxpr/reduce_scatter | solution.py:71
  242.8 5.0 collective-permute-done.1
  247.9 5.5 collective-permute-done.2
  253.4 5.5 collective-permute-done.3
  258.8 5.5 collective-permute-done.4
  264.4 5.5 collective-permute-done.5
  269.8 5.5 collective-permute-done.6
  280.6 13.9 %fusion.51 = f32[64,2048]{1,0:T(8,128)S(1)} fusion(f32[64,2048]{0,1:T(8,128)S(1)} %mul.87, f32[2048,2048]{1,0:T(8,128)} %get-tuple-element.499), kind=kOutput, calls=%fused_computation.59.clone.1 | convolution fusion | flops 3221225472 | bytes 17825792 | tf_op jit(solution)/shard_map/while/body/eval_jaxpr/dot_general | solution.py:57
  294.5 10.2 %fusion.52 = f32[64,2048]{1,0:T(8,128)S(1)} fusion(f32[64,2048]{0,1:T(8,128)S(1)} %mul.87, f32[2048,2048]{1,0:T(8,128)S(1)} %copy-done), kind=kOutput, calls=%fused_computation.58.clone.1 | convolution fusion | flops 3221225472 | bytes 17825792 | tf_op jit(solution)/shard_map/while/body/eval_jaxpr/dot_general | solution.py:56
  307.0 28.3 %reduce-scatter.2.cloned.1.call-done = f32[2,32,256]{2,1,0:T(8,128)} async-done(((f32[2,32,2048]{2,1,0:T(8,128)}), f32[2,32,256]{2,1,0:T(8,128)}) %reduce-scatter.2.cloned.1.call-update) | async-done | bytes 65552 | tf_op jit(solution)/shard_map/while/body/eval_jaxpr/reduce_scatter | solution.py:71
  347.5 5.0 collective-permute-done.1
  352.6 5.5 collective-permute-done.2
  358.0 5.5 collective-permute-done.3
  363.5 5.5 collective-permute-done.4
  369.0 5.5 collective-permute-done.5
  374.5 5.5 collective-permute-done.6
  385.3 13.9 %fusion.51 = f32[64,2048]{1,0:T(8,128)S(1)} fusion(f32[64,2048]{0,1:T(8,128)S(1)} %mul.87, f32[2048,2048]{1,0:T(8,128)} %get-tuple-element.499), kind=kOutput, calls=%fused_computation.59.clone.1 | convolution fusion | flops 3221225472 | bytes 17825792 | tf_op jit(solution)/shard_map/while/body/eval_jaxpr/dot_general | solution.py:57
  399.2 10.2 %fusion.52 = f32[64,2048]{1,0:T(8,128)S(1)} fusion(f32[64,2048]{0,1:T(8,128)S(1)} %mul.87, f32[2048,2048]{1,0:T(8,128)S(1)} %copy-done), kind=kOutput, calls=%fused_computation.58.clone.1 | convolution fusion | flops 3221225472 | bytes 17825792 | tf_op jit(solution)/shard_map/while/body/eval_jaxpr/dot_general | solution.py:56
  411.7 28.2 %reduce-scatter.2.cloned.1.call-done = f32[2,32,256]{2,1,0:T(8,128)} async-done(((f32[2,32,2048]{2,1,0:T(8,128)}), f32[2,32,256]{2,1,0:T(8,128)}) %reduce-scatter.2.cloned.1.call-update) | async-done | bytes 65552 | tf_op jit(solution)/shard_map/while/body/eval_jaxpr/reduce_scatter | solution.py:71
  452.1 5.1 collective-permute-done.1
  457.1 5.5 collective-permute-done.2
  462.6 5.5 collective-permute-done.3
  468.1 5.5 collective-permute-done.4
  473.6 5.5 collective-permute-done.5
  479.1 5.5 collective-permute-done.6
  489.8 13.9 %fusion.51 = f32[64,2048]{1,0:T(8,128)S(1)} fusion(f32[64,2048]{0,1:T(8,128)S(1)} %mul.87, f32[2048,2048]{1,0:T(8,128)} %get-tuple-element.499), kind=kOutput, calls=%fused_computation.59.clone.1 | convolution fusion | flops 3221225472 | bytes 17825792 | tf_op jit(solution)/shard_map/while/body/eval_jaxpr/dot_general | solution.py:57
  503.8 10.2 %fusion.52 = f32[64,2048]{1,0:T(8,128)S(1)} fusion(f32[64,2048]{0,1:T(8,128)S(1)} %mul.87, f32[2048,2048]{1,0:T(8,128)S(1)} %copy-done), kind=kOutput, calls=%fused_computation.58.clone.1 | convolution fusion | flops 3221225472 | bytes 17825792 | tf_op jit(solution)/shard_map/while/body/eval_jaxpr/dot_general | solution.py:56
  516.3 28.3 %reduce-scatter.2.cloned.1.call-done = f32[2,32,256]{2,1,0:T(8,128)} async-done(((f32[2,32,2048]{2,1,0:T(8,128)}), f32[2,32,256]{2,1,0:T(8,128)}) %reduce-scatter.2.cloned.1.call-update) | async-done | bytes 65552 | tf_op jit(solution)/shard_map/while/body/eval_jaxpr/reduce_scatter | solution.py:71
  556.8 5.0 collective-permute-done.1
  561.9 5.5 collective-permute-done.2
  567.4 5.5 collective-permute-done.3
  572.9 5.5 collective-permute-done.4
  578.4 5.5 collective-permute-done.5
  583.8 5.5 collective-permute-done.6
  594.6 13.9 %fusion.51 = f32[64,2048]{1,0:T(8,128)S(1)} fusion(f32[64,2048]{0,1:T(8,128)S(1)} %mul.87, f32[2048,2048]{1,0:T(8,128)} %get-tuple-element.499), kind=kOutput, calls=%fused_computation.59.clone.1 | convolution fusion | flops 3221225472 | bytes 17825792 | tf_op jit(solution)/shard_map/while/body/eval_jaxpr/dot_general | solution.py:57
  608.5 10.2 %fusion.52 = f32[64,2048]{1,0:T(8,128)S(1)} fusion(f32[64,2048]{0,1:T(8,128)S(1)} %mul.87, f32[2048,2048]{1,0:T(8,128)S(1)} %copy-done), kind=kOutput, calls=%fused_computation.58.clone.1 | convolution fusion | flops 3221225472 | bytes 17825792 | tf_op jit(solution)/shard_map/while/body/eval_jaxpr/dot_general | solution.py:56
  621.0 28.3 %reduce-scatter.2.cloned.1.call-done = f32[2,32,256]{2,1,0:T(8,128)} async-done(((f32[2,32,2048]{2,1,0:T(8,128)}), f32[2,32,256]{2,1,0:T(8,128)}) %reduce-scatter.2.cloned.1.call-update) | async-done | bytes 65552 | tf_op jit(solution)/shard_map/while/body/eval_jaxpr/reduce_scatter | solution.py:71
  661.5 5.0 collective-permute-done.1
  666.5 5.5 collective-permute-done.2
  672.0 5.5 collective-permute-done.3
  677.5 5.5 collective-permute-done.4
  683.0 5.5 collective-permute-done.5
  688.5 5.5 collective-permute-done.6
  699.2 13.9 %fusion.51 = f32[64,2048]{1,0:T(8,128)S(1)} fusion(f32[64,2048]{0,1:T(8,128)S(1)} %mul.87, f32[2048,2048]{1,0:T(8,128)} %get-tuple-element.499), kind=kOutput, calls=%fused_computation.59.clone.1 | convolution fusion | flops 3221225472 | bytes 17825792 | tf_op jit(solution)/shard_map/while/body/eval_jaxpr/dot_general | solution.py:57
  713.2 10.2 %fusion.52 = f32[64,2048]{1,0:T(8,128)S(1)} fusion(f32[64,2048]{0,1:T(8,128)S(1)} %mul.87, f32[2048,2048]{1,0:T(8,128)S(1)} %copy-done), kind=kOutput, calls=%fused_computation.58.clone.1 | convolution fusion | flops 3221225472 | bytes 17825792 | tf_op jit(solution)/shard_map/while/body/eval_jaxpr/dot_general | solution.py:56
  725.7 28.3 %reduce-scatter.2.cloned.1.call-done = f32[2,32,256]{2,1,0:T(8,128)} async-done(((f32[2,32,2048]{2,1,0:T(8,128)}), f32[2,32,256]{2,1,0:T(8,128)}) %reduce-scatter.2.cloned.1.call-update) | async-done | bytes 65552 | tf_op jit(solution)/shard_map/while/body/eval_jaxpr/reduce_scatter | solution.py:71
  760.0 18.5 %psum.7 = f32[1,2,4,32]{3,2,1,0:T(4,128)} all-reduce(f32[1,2,4,32]{3,2,1,0:T(4,128)S(1)} %bitcast.124), channel_id=1, replica_groups=mesh['section'=4,'stem'=8] {'stem'}, use_global_device_ids=true, to_apply=%region_4.5 | all-reduce | flops 256 | bytes 2048 | tf_op jit(solution)/shard_map/psum | solution.py:79
  (367 shorter events, 147.0 us)
Async XLA Ops:
  9.3 21.2 %copy-start.2 = (s32[1,4,32,3]{2,1,3,0:T(4,128)S(1)}, s32[1,4,32,3]{2,1,3,0:T(4,128)}, u32[]{:S(2)}) copy-start(s32[1,4,32,3]{2,1,3,0:T(4,128)} %param.7) | copy-start | bytes 4612
  30.6 95.3 %reduce-scatter.2.cloned.1.call-start = ((), (), s32[]{:S(2)}) async-start(), calls=%async_computation.1 | async-start | bytes 589824 | tf_op jit(solution)/shard_map/while/body/eval_jaxpr/reduce_scatter | solution.py:71
  30.7 3.2 collective-permute-start
  33.9 3.7 collective-permute-start.1
  37.6 5.5 collective-permute-start.2
  43.1 5.5 collective-permute-start.3
  48.6 5.5 collective-permute-start.4
  54.1 5.5 collective-permute-start.5
  59.6 5.5 collective-permute-start.6
  125.9 6.1 collective-permute-start.7
  132.1 98.6 %reduce-scatter.2.cloned.1.call-start = ((), (), s32[]{:S(2)}) async-start(), calls=%async_computation.1 | async-start | bytes 589824 | tf_op jit(solution)/shard_map/while/body/eval_jaxpr/reduce_scatter | solution.py:71
  132.1 5.7 collective-permute-start
  137.7 5.5 collective-permute-start.1
  143.2 5.5 collective-permute-start.2
  148.7 5.5 collective-permute-start.3
  154.2 5.5 collective-permute-start.4
  159.7 5.5 collective-permute-start.5
  165.2 5.5 collective-permute-start.6
  230.6 6.1 collective-permute-start.7
  236.7 98.6 %reduce-scatter.2.cloned.1.call-start = ((), (), s32[]{:S(2)}) async-start(), calls=%async_computation.1 | async-start | bytes 589824 | tf_op jit(solution)/shard_map/while/body/eval_jaxpr/reduce_scatter | solution.py:71
  236.7 5.7 collective-permute-start
  242.4 5.5 collective-permute-start.1
  247.9 5.5 collective-permute-start.2
  253.3 5.5 collective-permute-start.3
  258.8 5.5 collective-permute-start.4
  264.3 5.5 collective-permute-start.5
  269.8 5.5 collective-permute-start.6
  335.3 6.1 collective-permute-start.7
  341.4 98.4 %reduce-scatter.2.cloned.1.call-start = ((), (), s32[]{:S(2)}) async-start(), calls=%async_computation.1 | async-start | bytes 589824 | tf_op jit(solution)/shard_map/while/body/eval_jaxpr/reduce_scatter | solution.py:71
  341.4 5.7 collective-permute-start
  347.1 5.5 collective-permute-start.1
  352.5 5.5 collective-permute-start.2
  358.0 5.5 collective-permute-start.3
  363.5 5.5 collective-permute-start.4
  369.0 5.5 collective-permute-start.5
  374.5 5.5 collective-permute-start.6
  439.8 6.1 collective-permute-start.7
  445.9 98.7 %reduce-scatter.2.cloned.1.call-start = ((), (), s32[]{:S(2)}) async-start(), calls=%async_computation.1 | async-start | bytes 589824 | tf_op jit(solution)/shard_map/while/body/eval_jaxpr/reduce_scatter | solution.py:71
  445.9 5.7 collective-permute-start
  451.6 5.5 collective-permute-start.1
  457.1 5.5 collective-permute-start.2
  462.6 5.5 collective-permute-start.3
  468.1 5.5 collective-permute-start.4
  473.6 5.5 collective-permute-start.5
  479.1 5.5 collective-permute-start.6
  544.6 6.1 collective-permute-start.7
  550.7 98.5 %reduce-scatter.2.cloned.1.call-start = ((), (), s32[]{:S(2)}) async-start(), calls=%async_computation.1 | async-start | bytes 589824 | tf_op jit(solution)/shard_map/while/body/eval_jaxpr/reduce_scatter | solution.py:71
  550.7 5.7 collective-permute-start
  556.4 5.5 collective-permute-start.1
  561.9 5.5 collective-permute-start.2
  567.4 5.5 collective-permute-start.3
  572.8 5.5 collective-permute-start.4
  578.3 5.5 collective-permute-start.5
  583.8 5.5 collective-permute-start.6
  649.3 6.1 collective-permute-start.7
  655.4 98.5 %reduce-scatter.2.cloned.1.call-start = ((), (), s32[]{:S(2)}) async-start(), calls=%async_computation.1 | async-start | bytes 589824 | tf_op jit(solution)/shard_map/while/body/eval_jaxpr/reduce_scatter | solution.py:71
  655.4 5.7 collective-permute-start
  661.0 5.5 collective-permute-start.1
  666.5 5.5 collective-permute-start.2
  672.0 5.5 collective-permute-start.3
  677.5 5.5 collective-permute-start.4
  683.0 5.5 collective-permute-start.5
  688.5 5.5 collective-permute-start.6
  753.9 6.1 collective-permute-start.7
  (8 other events, 118.7 us)
Sparse Core Ops, SparseCore 0:
  95.5 30.3 reduce-scatter.1
  201.1 29.4 reduce-scatter.1
  305.8 29.4 reduce-scatter.1
  410.5 29.3 reduce-scatter.1
  515.0 29.5 reduce-scatter.1
  619.8 29.4 reduce-scatter.1
  724.4 29.4 reduce-scatter.1
